TPU v7x, 32 devices: a whole 2x2x4 slice. The times are simulated.
32 devices in a mesh: rows: 16 (over z, y, x), cols: 2 (over core).
Axes of the slice: x: 2, y: 2, z: 4, core: 2. Of those that a mesh axis runs over, the one named last changes fastest.
Arguments:
- embeddings: bfloat16 [49152, 1536], P('rows'), may hold values from -43 to 43, as said below
- start_basis: float32 [1536, 256], P(None, 'cols'), may hold values from -6 to 6
Outputs:
- projected: bfloat16 [49152, 256], P('rows', 'cols')
- basis: float32 [1536, 256], P(None, 'cols')
Inputs may be any that keep to these rules, and one draw needn't show every extreme that they name: `embeddings`: rows are noisy vectors around offsets that differ between aligned blocks of rows, with per-column spreads that differ by a factor of up to four.
All inputs are finite; a program needn't handle non-finite values.
Results may differ from a plain program's by a relative error of at most 0.025.
Values may be sent and summed in bfloat16 or wider, within the bound.
No kernel may reach another device: no remote copies, remote signals or barrier semaphores. Data moves between devices by JAX's collectives and lax.ppermute only.
A program may use at most 64 MiB of HBM per device.

v0:
```python
import jax
import jax.numpy as jnp
from jax import lax
from jax.sharding import PartitionSpec as P

K = 256
ITERS = 3


def shards(embeddings, start_basis):
    local_rows = embeddings.shape[0]
    col_block = start_basis.shape[1]
    col_start = lax.axis_index("cols") * col_block
    col_mean = lax.psum(jnp.sum(embeddings, axis=0, dtype=jnp.float32), "rows")
    col_mean = col_mean / (local_rows * lax.axis_size("rows"))
    basis = start_basis
    for sweep_index in range(ITERS):
        basis_bf = basis.astype(jnp.bfloat16)
        raw_proj = jnp.dot(embeddings, basis_bf, preferred_element_type=jnp.float32)
        offset = jnp.dot(col_mean, basis_bf.astype(jnp.float32), precision=lax.Precision.HIGHEST)
        shifted = (raw_proj - offset[None, :]).astype(jnp.bfloat16)
        local_sums = jnp.sum(shifted, axis=0, dtype=jnp.float32)
        partial_products = lax.dot_general(
            embeddings, shifted, (((0,), (0,)), ((), ())), preferred_element_type=jnp.float32
        )
        summed, col_sums = lax.psum((partial_products, local_sums), "rows")
        products = summed - col_mean[:, None] * col_sums[None, :]
        full_products = lax.all_gather(
            products.astype(jnp.bfloat16), "cols", axis=1, tiled=True
        ).astype(products.dtype)
        gram_matrix = jnp.dot(full_products.T, full_products, precision=lax.Precision.HIGHEST)
        lower = jnp.linalg.cholesky(gram_matrix)
        solved = lax.linalg.triangular_solve(
            lower, full_products, left_side=False, lower=True, transpose_a=True
        )
        basis = lax.dynamic_slice_in_dim(solved, col_start, col_block, 1)
    centered = embeddings.astype(jnp.float32) - col_mean[None, :]
    unit = (centered * lax.rsqrt(jnp.sum(centered * centered, axis=1, keepdims=True) + 1.0)).astype(
        jnp.bfloat16
    )
    coords = jnp.dot(unit, basis.astype(jnp.bfloat16), preferred_element_type=jnp.float32)
    squares = lax.psum(jnp.sum(coords * coords, axis=1), "cols")
    scaled = coords * lax.rsqrt(squares[:, None] / K + 0.0001)
    return (scaled.astype(jnp.bfloat16), basis)


def solution(mesh):
    in_specs = (P("rows", None), P(None, "cols"))
    out_specs = (P("rows", "cols"), P(None, "cols"))
    return jax.shard_map(shards, mesh=mesh, in_specs=in_specs, out_specs=out_specs, check_vma=False)
```

profile of v0, /device:TPU:0, one launch (start us, length us, event | category | flops | bytes accessed | tf_op | source)
XLA Modules:
  0.0 638.1 jit_solution(6976199507858413870)
XLA Ops:
  7.2 5.1 convert_reduce_fusion
  12.3 44.0 %psum.56 = f32[1536]{0:T(1024)S(1)} all-reduce(f32[1536]{0:T(1024)S(1)} %convert_reduce_fusion), channel_id=1, replica_groups=mesh['rows'=16,'cols'=2] {'rows'}, use_global_device_ids=true, to_apply=%region_1.0 | all-reduce | flops 1536 | bytes 12288 | tf_op jit(solution)/shard_map/psum | solution.py:14
  56.6 6.3 convert_reduce_fusion.3
  63.0 6.0 convolution_bitcast_fusion.2
  69.0 36.9 %psum.58 = f32[128]{0:T(128)S(1)} all-reduce(f32[128]{0:T(128)S(1)} %get-tuple-element.71), channel_id=1, replica_groups=mesh['rows'=16,'cols'=2] {'rows'}, use_global_device_ids=true, to_apply=%region_5.6 | all-reduce | flops 128 | bytes 1024 | tf_op jit(solution)/shard_map/psum | solution.py:26
  105.9 69.9 %all-reduce.5.cloned.1.call-done = f32[1536,128]{0,1:T(8,128)} async-done(((f32[1536,128]{0,1:T(8,128)}), f32[1536,128]{0,1:T(8,128)}) %all-reduce.5.cloned.1.call-update) | async-done | bytes 786448 | tf_op jit(solution)/shard_map/psum | solution.py:26
  180.4 11.7 %cholesky.172 = f32[128,128]{1,0:T(8,128)S(1)} custom-call(f32[128,128]{1,0:T(8,128)S(1)} %cholesky.270), custom_call_target="Cholesky" | custom-call | tf_op jit(solution)/shard_map/jit(cholesky)/cholesky | solution.py:32
  192.2 9.8 %custom-call.15 = f32[1,128,128]{1,2,0:T(8,128)S(1)} custom-call(f32[1,128,128]{2,1,0:T(8,128)S(1)} %get-tuple-element.70), custom_call_target="InvertDiagBlocksLowerTriangular" | custom-call | tf_op jit(solution)/shard_map/jit(cholesky)/cholesky | solution.py:32
  202.5 11.7 %cholesky.189 = f32[128,128]{1,0:T(8,128)S(1)} custom-call(f32[128,128]{1,0:T(8,128)S(1)} %convolution_subtract_fusion.8), custom_call_target="Cholesky" | custom-call | tf_op jit(solution)/shard_map/jit(cholesky)/cholesky | solution.py:32
  216.4 4.3 while.6
  220.8 19.7 %custom-call.16 = f32[2,128,128]{1,2,0:T(8,128)S(1)} custom-call(f32[2,128,128]{2,1,0:T(8,128)S(1)} %get-tuple-element.24), custom_call_target="InvertDiagBlocksLowerTriangular" | custom-call | tf_op jit(solution)/shard_map/triangular_solve/custom-call.0 | solution.py:33
  243.6 7.1 %convert_reduce_fusion.2 = (f32[128]{0:T(128)S(1)}, bf16[128,3072]{1,0:T(8,128)(2,1)S(1)}) fusion(f32[128]{0:T(128)S(1)} %convolution_bitcast_fusion.4, bf16[1536,128]{0,1:T(8,128)(2,1)S(1)} %fusion.15, bf16[3072,1536]{1,0:T(8,128)(2,1)} %param.5), kind=kOutput, calls=%fused_computation.36 | convolution fusion | flops 1209532288 | bytes 10617856 | tf_op jit(solution)/shard_map/dot_general | solution.py:19
  253.1 39.9 %psum.60 = f32[128]{0:T(128)S(1)} all-reduce(f32[128]{0:T(128)S(1)} %get-tuple-element.75), channel_id=1, replica_groups=mesh['rows'=16,'cols'=2] {'rows'}, use_global_device_ids=true, to_apply=%region_12.15 | all-reduce | flops 128 | bytes 1024 | tf_op jit(solution)/shard_map/psum | solution.py:26
  292.9 70.4 %all-reduce.7.cloned.1.call-done = f32[1536,128]{0,1:T(8,128)} async-done(((f32[1536,128]{0,1:T(8,128)}), f32[1536,128]{0,1:T(8,128)}) %all-reduce.7.cloned.1.call-update) | async-done | bytes 786448 | tf_op jit(solution)/shard_map/psum | solution.py:26
  364.6 2.8 all_gather.10
  368.2 11.7 %cholesky.206 = f32[128,128]{1,0:T(8,128)S(1)} custom-call(f32[128,128]{1,0:T(8,128)S(1)} %cholesky.273), custom_call_target="Cholesky" | custom-call | tf_op jit(solution)/shard_map/jit(cholesky)/cholesky | solution.py:32
  380.0 9.8 %custom-call.17 = f32[1,128,128]{1,2,0:T(8,128)S(1)} custom-call(f32[1,128,128]{2,1,0:T(8,128)S(1)} %get-tuple-element.66), custom_call_target="InvertDiagBlocksLowerTriangular" | custom-call | tf_op jit(solution)/shard_map/jit(cholesky)/cholesky | solution.py:32
  390.3 11.7 %cholesky.223 = f32[128,128]{1,0:T(8,128)S(1)} custom-call(f32[128,128]{1,0:T(8,128)S(1)} %convolution_subtract_fusion.7), custom_call_target="Cholesky" | custom-call | tf_op jit(solution)/shard_map/jit(cholesky)/cholesky | solution.py:32
  404.8 4.3 while.7
  409.1 19.7 %custom-call.18 = f32[2,128,128]{1,2,0:T(8,128)S(1)} custom-call(f32[2,128,128]{2,1,0:T(8,128)S(1)} %get-tuple-element.25), custom_call_target="InvertDiagBlocksLowerTriangular" | custom-call | tf_op jit(solution)/shard_map/triangular_solve/custom-call.0 | solution.py:33
  431.9 7.1 %convert_reduce_fusion.1 = (f32[128]{0:T(128)S(1)}, bf16[128,3072]{1,0:T(8,128)(2,1)S(1)}) fusion(f32[128]{0:T(128)S(1)} %convolution_bitcast_fusion.3, bf16[1536,128]{0,1:T(8,128)(2,1)S(1)} %fusion.13, bf16[3072,1536]{1,0:T(8,128)(2,1)} %param.5), kind=kOutput, calls=%fused_computation.35 | convolution fusion | flops 1209532288 | bytes 10617856 | tf_op jit(solution)/shard_map/dot_general | solution.py:19
  441.3 6.2 fusion.2
  447.5 39.8 %psum.62 = f32[128]{0:T(128)S(1)} all-reduce(f32[128]{0:T(128)S(1)} %get-tuple-element.79), channel_id=1, replica_groups=mesh['rows'=16,'cols'=2] {'rows'}, use_global_device_ids=true, to_apply=%region_15.18 | all-reduce | flops 128 | bytes 1024 | tf_op jit(solution)/shard_map/psum | solution.py:26
  487.3 64.2 %all-reduce.9.cloned.1.call-done = f32[1536,128]{0,1:T(8,128)} async-done(((f32[1536,128]{0,1:T(8,128)}), f32[1536,128]{0,1:T(8,128)}) %all-reduce.9.cloned.1.call-update) | async-done | bytes 786448 | tf_op jit(solution)/shard_map/psum | solution.py:26
  552.8 2.6 all_gather.11
  556.2 11.7 %cholesky.240 = f32[128,128]{1,0:T(8,128)S(1)} custom-call(f32[128,128]{1,0:T(8,128)S(1)} %cholesky.276), custom_call_target="Cholesky" | custom-call | tf_op jit(solution)/shard_map/jit(cholesky)/cholesky | solution.py:32
  567.9 9.8 %custom-call.19 = f32[1,128,128]{1,2,0:T(8,128)S(1)} custom-call(f32[1,128,128]{2,1,0:T(8,128)S(1)} %get-tuple-element.62), custom_call_target="InvertDiagBlocksLowerTriangular" | custom-call | tf_op jit(solution)/shard_map/jit(cholesky)/cholesky | solution.py:32
  578.2 11.7 %cholesky.257 = f32[128,128]{1,0:T(8,128)S(1)} custom-call(f32[128,128]{1,0:T(8,128)S(1)} %convolution_subtract_fusion.6), custom_call_target="Cholesky" | custom-call | tf_op jit(solution)/shard_map/jit(cholesky)/cholesky | solution.py:32
  592.7 4.4 while.8
  597.1 19.7 %custom-call.20 = f32[2,128,128]{1,2,0:T(8,128)S(1)} custom-call(f32[2,128,128]{2,1,0:T(8,128)S(1)} %get-tuple-element.26), custom_call_target="InvertDiagBlocksLowerTriangular" | custom-call | tf_op jit(solution)/shard_map/triangular_solve/custom-call.0 | solution.py:33
  620.7 6.0 multiply_reduce_fusion
  626.7 3.3 psum.63
  (111 shorter events, 42.5 us)
Async XLA Ops:
  7.2 49.2 %copy-start = (f32[1536,128]{1,0:T(8,128)S(1)}, f32[1536,128]{1,0:T(8,128)}, u32[]{:S(2)}) copy-start(f32[1536,128]{1,0:T(8,128)} %param.6) | copy-start | bytes 2359300
  7.2 168.7 %all-reduce.5.cloned.1.call-start = ((), (), s32[]{:S(2)}) async-start(), calls=%async_computation | async-start | bytes 1572864 | tf_op jit(solution)/shard_map/psum | solution.py:26
  69.0 294.4 %all-reduce.7.cloned.1.call-start = ((), (), s32[]{:S(2)}) async-start(), calls=%async_computation.1 | async-start | bytes 1572864 | tf_op jit(solution)/shard_map/psum | solution.py:26
  180.4 70.3 %slice-start = ((s8[9437184]{0:T(1024)(128)(4,1)}), s8[1048576]{0:T(1024)(128)(4,1)S(1)}, s32[]{:S(2)}) async-start(s8[9437184]{0:T(1024)(128)(4,1)} %bitcast.130), calls=%async_computation.3 | async-start | bytes 2097152
  241.3 9.4 %slice-start.1 = ((s8[9437184]{0:T(1024)(128)(4,1)}), s8[4194304]{0:T(1024)(128)(4,1)S(1)}, s32[]{:S(2)}) async-start(s8[9437184]{0:T(1024)(128)(4,1)} %bitcast.130), calls=%async_computation.4 | async-start | bytes 8388608
  243.6 7.1 %slice-start.2 = ((s8[9437184]{0:T(1024)(128)(4,1)}), s8[4194304]{0:T(1024)(128)(4,1)S(1)}, s32[]{:S(2)}) async-start(s8[9437184]{0:T(1024)(128)(4,1)} %bitcast.130), calls=%async_computation.5 | async-start | bytes 8388608
  253.0 298.5 %all-reduce.9.cloned.1.call-start = ((), (), s32[]{:S(2)}) async-start(), calls=%async_computation.2 | async-start | bytes 1572864 | tf_op jit(solution)/shard_map/psum | solution.py:26
  368.1 70.8 %slice-start.3 = ((s8[9437184]{0:T(1024)(128)(4,1)}), s8[1048576]{0:T(1024)(128)(4,1)S(1)}, s32[]{:S(2)}) async-start(s8[9437184]{0:T(1024)(128)(4,1)} %bitcast.132), calls=%async_computation.6 | async-start | bytes 2097152
  429.6 9.4 %slice-start.4 = ((s8[9437184]{0:T(1024)(128)(4,1)}), s8[4194304]{0:T(1024)(128)(4,1)S(1)}, s32[]{:S(2)}) async-start(s8[9437184]{0:T(1024)(128)(4,1)} %bitcast.132), calls=%async_computation.7 | async-start | bytes 8388608
  431.9 7.1 %slice-start.5 = ((s8[9437184]{0:T(1024)(128)(4,1)}), s8[4194304]{0:T(1024)(128)(4,1)S(1)}, s32[]{:S(2)}) async-start(s8[9437184]{0:T(1024)(128)(4,1)} %bitcast.132), calls=%async_computation.8 | async-start | bytes 8388608
Sparse Core Ops, SparseCore 0:
  69.1 106.6 all-reduce.4
  253.1 110.1 all-reduce.6
  441.5 110.0 all-reduce.8
where the time goes:
time: 643 us; the launch traced here: 638 us
  waiting for transfers between devices  205 us (32%)
  other arithmetic  179 us (28%)
  blocking collectives  172 us (27%)
  matrix products  48.3 us (8%)
  between operations  18.6 us (3%)
  local copies, waits for them, and re-layouts  15.1 us (2%)
    psum x3, waiting for transfers between devices, shards(): summed, col_sums = lax.psum((partial_products, local_sums), 'rows')  205 us
    psum x3, blocking collectives, shards(): summed, col_sums = lax.psum((partial_products, local_sums), 'rows')  117 us
    another operation x20, other arithmetic, shards(): lower = jnp.linalg.cholesky(gram_matrix)  103 us
    another operation x8, other arithmetic, shards(): lax.linalg.triangular_solve(lower, full_products, left_side=False, lower=...  59.3 us
    psum x1, blocking collectives, shards(): col_mean = lax.psum(jnp.sum(embeddings, axis=0, dtype=jnp.float32), 'rows')  44 us
    dot_general x3, matrix products, shards(): raw_proj = jnp.dot(embeddings, basis_bf, preferred_element_type=jnp.float32)  20.5 us
  transfers between devices with their start and end apart: 3, of which 3 were waited for; matrix products, arithmetic and copies ran while one was open for 1% of the time, Pallas kernels for 0%

commit v1 on v0

v1 whole, which is shorter than its diff:
```python
import jax
import jax.numpy as jnp
from jax import lax
from jax.experimental import pallas as pl
from jax.experimental.pallas import tpu as pltpu
from jax.sharding import PartitionSpec as P

ITERS = 3
PANEL = 16
LANES = 128


def split3(x):
    hi = x.astype(jnp.bfloat16)
    rest = x - hi.astype(jnp.float32)
    mid = rest.astype(jnp.bfloat16)
    low = (rest - mid.astype(jnp.float32)).astype(jnp.bfloat16)
    return hi, mid, low


def inverse_factor_kernel(gram_ref, inv_ref, work_ref):
    size = gram_ref.shape[0]
    work_ref[...] = gram_ref[...]
    row = lax.broadcasted_iota(jnp.int32, (size, size), 0)
    col = lax.broadcasted_iota(jnp.int32, (size, size), 1)
    inv_ref[...] = (row == col).astype(jnp.float32)
    sub = lax.broadcasted_iota(jnp.int32, (PANEL, LANES), 0)
    chunks = size // LANES
    for start in range(0, size, PANEL):
        end = start + PANEL
        block = work_ref[start:end, :]
        first = start // LANES
        pieces = [work_ref[start:end, c * LANES : (c + 1) * LANES] for c in range(first, chunks)]
        count = len(pieces)
        pieces += [inv_ref[start:end, c * LANES : (c + 1) * LANES] for c in range(first + 1)]
        spread = [jnp.broadcast_to(block[:, start + k : start + k + 1], (PANEL, LANES)) for k in range(PANEL)]
        scale = jnp.ones((PANEL, LANES), jnp.float32)
        for k in range(PANEL):
            pivot = spread[k][k : k + 1, :]
            scale = jnp.where(sub == k, lax.rsqrt(pivot), scale)
            if k + 1 < PANEL:
                factor = jnp.where(sub > k, spread[k] * (1.0 / pivot), 0.0)
                pieces = [x - factor * x[k : k + 1, :] for x in pieces]
                spread = [x if i <= k else x - factor * x[k : k + 1, :] for i, x in enumerate(spread)]
        pieces = [x * scale for x in pieces]
        for i, c in enumerate(range(first + 1)):
            inv_ref[start:end, c * LANES : (c + 1) * LANES] = pieces[count + i]
        if end < size:
            hi, mid, low = split3(jnp.concatenate(pieces, axis=1))
            left = jnp.concatenate([hi, hi, mid, hi, low, mid], axis=0)[:, : count * LANES]
            right = jnp.concatenate([hi, mid, hi, low, hi, mid], axis=0)
            change = lax.dot_general(left, right, (((0,), (0,)), ((), ())), preferred_element_type=jnp.float32)
            change = change[end - first * LANES :, :]
            work_ref[end:, first * LANES :] = work_ref[end:, first * LANES :] - change[:, : count * LANES]
            done = (first + 1) * LANES
            inv_ref[end:, :done] = inv_ref[end:, :done] - change[:, count * LANES :]


def inverse_factor(gram):
    return pl.pallas_call(
        inverse_factor_kernel,
        out_shape=jax.ShapeDtypeStruct(gram.shape, jnp.float32),
        scratch_shapes=[pltpu.VMEM(gram.shape, jnp.float32)],
    )(gram)


def gather_rows(x):
    parts = lax.axis_size("rows")
    copies = jnp.broadcast_to(x[None], (parts,) + x.shape)
    return lax.all_to_all(copies, "rows", 0, 0)


def shards(embeddings, start_basis):
    f32, bf16 = jnp.float32, jnp.bfloat16
    local_rows, width = embeddings.shape
    row_parts = lax.axis_size("rows")
    col_parts = lax.axis_size("cols")
    row_index = lax.axis_index("rows")
    col_index = lax.axis_index("cols")
    col_block = start_basis.shape[1]
    basis_cols = col_block * col_parts
    half = width // col_parts
    piece = half // row_parts
    highest = lax.Precision.HIGHEST

    own_mean = jnp.sum(embeddings, axis=0, dtype=f32) / local_rows
    means = gather_rows(own_mean[None, :])[:, 0, :]
    col_mean = jnp.mean(means, axis=0)

    own_half = lax.dynamic_slice_in_dim(embeddings, col_index * half, half, 1)
    own_half_mean = lax.dynamic_slice_in_dim(own_mean, col_index * half, half, 0)
    second = lax.dot_general(own_half, embeddings, (((0,), (0,)), ((), ())), preferred_element_type=f32)
    within = (second - (local_rows * own_half_mean)[:, None] * own_mean[None, :]).astype(bf16)
    received = lax.all_to_all(within.reshape(row_parts, piece, width), "rows", 0, 0)
    between = means - col_mean[None, :]
    own_between = lax.dynamic_slice_in_dim(between, col_index * half + row_index * piece, piece, 1)
    scatter = jnp.sum(received.astype(f32), axis=0) + local_rows * lax.dot_general(
        own_between, between, (((0,), (0,)), ((), ())), precision=highest
    )

    basis = lax.all_gather(start_basis.astype(bf16), "cols", axis=1, tiled=True)
    next_piece = jnp.dot(scatter, basis.astype(f32), precision=highest)
    for sweep_index in range(ITERS):
        own_products = gather_rows(next_piece.astype(bf16)).reshape(half, basis_cols)
        products = lax.all_gather(own_products, "cols", axis=0, tiled=True)
        gram_matrix = lax.dot_general(products, products, (((0,), (0,)), ((), ())), preferred_element_type=f32)
        inverse = inverse_factor(gram_matrix)
        if sweep_index + 1 < ITERS:
            mixed = jnp.dot(scatter, products.astype(f32), precision=highest)
            next_piece = lax.dot_general(mixed, inverse, (((1,), (1,)), ((), ())), precision=highest)
    basis = lax.dot_general(products.astype(f32), inverse, (((1,), (1,)), ((), ())), precision=highest)

    centered = embeddings.astype(f32) - col_mean[None, :]
    unit = (centered * lax.rsqrt(jnp.sum(centered * centered, axis=1, keepdims=True) + 1.0)).astype(bf16)
    coords = jnp.dot(unit, basis.astype(bf16), preferred_element_type=f32)
    squares = jnp.sum(coords * coords, axis=1, keepdims=True)
    own_coords = lax.dynamic_slice_in_dim(coords, col_index * col_block, col_block, 1)
    scaled = own_coords * lax.rsqrt(squares / basis_cols + 0.0001)
    own_basis = lax.dynamic_slice_in_dim(basis, col_index * col_block, col_block, 1)
    return (scaled.astype(bf16), own_basis)


def solution(mesh):
    in_specs = (P("rows", None), P(None, "cols"))
    out_specs = (P("rows", "cols"), P(None, "cols"))
    return jax.shard_map(shards, mesh=mesh, in_specs=in_specs, out_specs=out_specs, check_vma=False)
```

time: 643 us -> 194 us (0.30)
  other arithmetic: 179 us -> 13.7 us
  waiting for transfers between devices: 205 us -> 62.5 us
  blocking collectives: 172 us -> 32.2 us
  Pallas kernels: 0 us -> 27.6 us
  starting transfers between devices: 0.12 us -> 22.7 us
  matrix products: 48.3 us -> 28.8 us
  between operations: 18.6 us -> 0.82 us
  local copies, waits for them, and re-layouts: 15.1 us -> 5 us
    psum x3 -> x0, waiting for transfers between devices: 205 us -> none  [shards(): summed, col_sums = lax.psum((partial_products, local_sums), 'rows')]
    psum x5 -> x0, blocking collectives: 164 us -> none  [the longest x3 117 us: shards(): summed, col_sums = lax.psum((partial_products, local_sums), 'rows')]
    another operation x28 -> x0, other arithmetic: 163 us -> none  [the longest x20 103 us: shards(): lower = jnp.linalg.cholesky(gram_matrix)]
    all_to_all x0 -> x4, waiting for transfers between devices: none -> 62.5 us  [the longest x1 42.8 us: shards(): lax.all_to_all(within.reshape(row_parts, piece, width), 'rows', 0, 0)]
    pallas_call x0 -> x3, Pallas kernels: none -> 27.6 us  [inverse_factor(): pl.pallas_call(inverse_factor_kernel, out_shape=jax.ShapeDtypeStruct(gram...]
    all_to_all x0 -> x4, starting transfers between devices: none -> 22.7 us  [the longest x3 15.8 us: gather_rows(): return lax.all_to_all(copies, 'rows', 0, 0)]
    all_to_all x0 -> x1, blocking collectives: none -> 22.6 us  [gather_rows(): return lax.all_to_all(copies, 'rows', 0, 0)]
    another operation x28 -> x0, local copies, waits for them, and re-layouts: 12.3 us -> none  [the longest x22 12.3 us: shards(): lax.linalg.triangular_solve(lower, full_products, left_side=False, lower=...]
  transfers between devices with their start and end apart: 3 -> 4, of which waited for: 3 -> 3; matrix products, arithmetic and copies ran while one was open for 1% -> 11% of each run, Pallas kernels for 0% -> 0%
where the time goes in v1:
time: 194 us; the launch traced here: 193 us
  waiting for transfers between devices  62.5 us (32%)
  blocking collectives  32.2 us (17%)
  matrix products  28.8 us (15%)
  Pallas kernels  27.6 us (14%)
  starting transfers between devices  22.7 us (12%)
  other arithmetic  13.7 us (7%)
  local copies, waits for them, and re-layouts  5 us (3%)
    all_to_all x1, waiting for transfers between devices, shards(): lax.all_to_all(within.reshape(row_parts, piece, width), 'rows', 0, 0)  42.8 us
    pallas_call x3, Pallas kernels, inverse_factor(): pl.pallas_call(inverse_factor_kernel, out_shape=jax.ShapeDtypeStruct(gram...  27.6 us
    all_to_all x1, blocking collectives, gather_rows(): return lax.all_to_all(copies, 'rows', 0, 0)  22.6 us
    all_to_all x3, waiting for transfers between devices, gather_rows(): return lax.all_to_all(copies, 'rows', 0, 0)  19.7 us
    all_to_all x3, starting transfers between devices, gather_rows(): return lax.all_to_all(copies, 'rows', 0, 0)  15.8 us
    dot_general x1, matrix products, shards(): lax.dot_general(own_half, embeddings, (((0,), (0,)), ((), ())), preferred...  12.7 us
    all_gather x3, blocking collectives, shards(): products = lax.all_gather(own_products, 'cols', axis=0, tiled=True)  7.25 us
    all_to_all x1, starting transfers between devices, shards(): lax.all_to_all(within.reshape(row_parts, piece, width), 'rows', 0, 0)  6.9 us
  transfers between devices with their start and end apart: 4, of which 3 were waited for; matrix products, arithmetic and copies ran while one was open for 11% of the time, Pallas kernels for 0%

profile of v1, /device:TPU:0, one launch (start us, length us, event | category | flops | bytes accessed | tf_op | source)
XLA Modules:
  0.0 193.3 jit_solution(15015621820199759313)
XLA Ops:
  0.6 5.0 %convert_reduce_fusion = f32[1536]{0:T(1024)S(1)} fusion(bf16[3072,1536]{1,0:T(8,128)(2,1)} %param.2), kind=kLoop, calls=%fused_computation.1 | loop fusion | flops 9435648 | bytes 9443328 | tf_op jit(solution)/shard_map/reduce_sum | solution.py:86
  5.7 0.7 broadcast_in_dim.8
  6.3 8.3 %all-to-all-start = ((f32[16,1,1536]{2,1,0:T(1,128)}), f32[16,1,1536]{2,1,0:T(1,128)S(1)}, u32[]{:S(2)}, u32[]{:S(2)}) async-start(f32[16,1,1536]{2,1,0:T(1,128)} %broadcast_in_dim.8), calls=%async_computation | async-start | bytes 196608 | tf_op jit(solution)/shard_map/all_to_all | solution.py:70
  14.8 12.7 %subtract_convert_fusion = bf16[768,1536]{1,0:T(8,128)(2,1)} fusion(bf16[3072,1536]{1,0:T(8,128)(2,1)} %param.2, s32[]{:T(128)S(6)} %select_n.11, f32[1536]{0:T(1024)S(1)} %broadcast_multiply_fusion.1, f32[768]{0:T(1024)S(1)} %dynamic-slice_multiply_fusion), kind=kOutput, calls=%fused_computation.10 | convolution fusion | flops 7251296256 | bytes 16524292 | tf_op jit(solution)/shard_map/dot_general | solution.py:92
  28.1 6.9 %all-to-all-start.1 = ((bf16[16,48,1536]{2,1,0:T(8,128)(2,1)}), bf16[16,48,1536]{2,1,0:T(8,128)(2,1)S(1)}, u32[]{:S(2)}, u32[]{:S(2)}) async-start(bf16[16,48,1536]{2,1,0:T(8,128)(2,1)} %bitcast.26), calls=%async_computation.1 | async-start | bytes 4718592 | tf_op jit(solution)/shard_map/all_to_all | solution.py:94
  35.1 2.4 %all_gather.12 = bf16[1536,256]{1,0:T(8,128)(2,1)S(1)} all-gather(bf16[1536,128]{1,0:T(8,128)(2,1)S(1)} %convert_element_type.39), channel_id=1, replica_groups=mesh['rows'=16,'cols'=2] {'cols'}, dimensions={1}, use_global_device_ids=true | all-gather | bytes 1179648 | tf_op jit(solution)/shard_map/all_gather | solution.py:101
  37.5 1.0 reduce_sum.46
  38.5 0.9 bitcast_subtract_fusion
  39.4 42.8 %all-to-all-done.1 = bf16[16,48,1536]{2,1,0:T(8,128)(2,1)S(1)} async-done(((bf16[16,48,1536]{2,1,0:T(8,128)(2,1)}), bf16[16,48,1536]{2,1,0:T(8,128)(2,1)S(1)}, u32[]{:S(2)}, u32[]{:S(2)}) %all-to-all-start.1) | async-done | bytes 2359328 | tf_op jit(solution)/shard_map/all_to_all | solution.py:94
  83.6 22.6 %all_to_all.25 = bf16[16,48,256]{2,1,0:T(8,128)(2,1)S(1)} all-to-all(bf16[16,48,256]{2,1,0:T(8,128)(2,1)S(1)} %broadcast_in_dim.9), channel_id=1, replica_groups=mesh['rows'=16,'cols'=2] {'rows'}, dimensions={0} | all-to-all | bytes 786432 | tf_op jit(solution)/shard_map/all_to_all | solution.py:70
  106.2 2.5 %all_gather.13 = bf16[1536,256]{1,0:T(8,128)(2,1)S(1)} all-gather(bf16[768,256]{1,0:T(8,128)(2,1)S(1)} %bitcast.29), channel_id=1, replica_groups=mesh['rows'=16,'cols'=2] {'cols'}, dimensions={0}, use_global_device_ids=true | all-gather | bytes 1179648 | tf_op jit(solution)/shard_map/all_gather | solution.py:105
  109.2 1.1 fusion.18.gram_ref
  110.3 9.2 %shard_map.41 = f32[256,256]{1,0:T(8,128)} custom-call(f32[256,256]{1,0:T(8,128)} %fusion.18.gram_ref), custom_call_target="tpu_custom_call" | custom-call | tf_op jit(solution)/shard_map/pallas_call | solution.py:60
  119.5 1.3 convolution_convert_fusion.1
  120.8 0.8 broadcast_in_dim.10
  121.6 3.6 %all-to-all-start.3 = ((bf16[16,48,256]{2,1,0:T(8,128)(2,1)}), bf16[16,48,256]{2,1,0:T(8,128)(2,1)S(1)}, u32[]{:S(2)}, u32[]{:S(2)}) async-start(bf16[16,48,256]{2,1,0:T(8,128)(2,1)} %broadcast_in_dim.10), calls=%async_computation.3 | async-start | bytes 786432 | tf_op jit(solution)/shard_map/all_to_all | solution.py:70
  125.3 13.0 %all-to-all-done.3 = bf16[16,48,256]{2,1,0:T(8,128)(2,1)S(1)} async-done(((bf16[16,48,256]{2,1,0:T(8,128)(2,1)}), bf16[16,48,256]{2,1,0:T(8,128)(2,1)S(1)}, u32[]{:S(2)}, u32[]{:S(2)}) %all-to-all-start.3) | async-done | bytes 393248 | tf_op jit(solution)/shard_map/all_to_all | solution.py:70
  138.3 2.4 %all_gather.14 = bf16[1536,256]{1,0:T(8,128)(2,1)S(1)} all-gather(bf16[768,256]{1,0:T(8,128)(2,1)S(1)} %bitcast.27), channel_id=1, replica_groups=mesh['rows'=16,'cols'=2] {'cols'}, dimensions={0}, use_global_device_ids=true | all-gather | bytes 1179648 | tf_op jit(solution)/shard_map/all_gather | solution.py:105
  140.7 1.1 fusion.20.gram_ref
  142.3 9.2 %shard_map.42 = f32[256,256]{1,0:T(8,128)} custom-call(f32[256,256]{1,0:T(8,128)} %fusion.20.gram_ref), custom_call_target="tpu_custom_call" | custom-call | tf_op jit(solution)/shard_map/pallas_call | solution.py:60
  151.5 1.3 convolution_convert_fusion
  152.8 0.8 broadcast_in_dim.11
  153.6 3.8 %all-to-all-start.4 = ((bf16[16,48,256]{2,1,0:T(8,128)(2,1)}), bf16[16,48,256]{2,1,0:T(8,128)(2,1)S(1)}, u32[]{:S(2)}, u32[]{:S(2)}) async-start(bf16[16,48,256]{2,1,0:T(8,128)(2,1)} %broadcast_in_dim.11), calls=%async_computation.4 | async-start | bytes 786432 | tf_op jit(solution)/shard_map/all_to_all | solution.py:70
  157.4 6.2 %fusion.2 = f32[3072]{0:T(1024)S(1)} fusion(bf16[3072,1536]{1,0:T(8,128)(2,1)} %param.2, f32[1536]{0:T(1024)S(1)} %broadcast_multiply_fusion), kind=kLoop, calls=%fused_computation.4 | loop fusion | flops 18871296 | bytes 9455616 | tf_op jit(solution)/shard_map/reduce_sum | solution.py:114
  163.6 6.7 %all-to-all-done.4 = bf16[16,48,256]{2,1,0:T(8,128)(2,1)S(1)} async-done(((bf16[16,48,256]{2,1,0:T(8,128)(2,1)}), bf16[16,48,256]{2,1,0:T(8,128)(2,1)S(1)}, u32[]{:S(2)}, u32[]{:S(2)}) %all-to-all-start.4) | async-done | bytes 393248 | tf_op jit(solution)/shard_map/all_to_all | solution.py:70
  170.2 2.4 %all_gather.15 = bf16[1536,256]{1,0:T(8,128)(2,1)S(1)} all-gather(bf16[768,256]{1,0:T(8,128)(2,1)S(1)} %bitcast.28), channel_id=1, replica_groups=mesh['rows'=16,'cols'=2] {'cols'}, dimensions={0}, use_global_device_ids=true | all-gather | bytes 1179648 | tf_op jit(solution)/shard_map/all_gather | solution.py:105
  172.6 1.1 fusion.21.gram_ref
  173.7 9.2 %shard_map.43 = f32[256,256]{1,0:T(8,128)} custom-call(f32[256,256]{1,0:T(8,128)} %fusion.21.gram_ref), custom_call_target="tpu_custom_call" | custom-call | tf_op jit(solution)/shard_map/pallas_call | solution.py:60
  182.9 1.8 fusion.22
  184.7 6.3 %multiply_reduce_fusion = (f32[3072]{0:T(1024)S(1)}, f32[3072,256]{0,1:T(8,128)S(1)}) fusion(f32[1536,256]{1,0:T(8,128)S(1)} %fusion.22, bf16[3072,1536]{1,0:T(8,128)(2,1)} %param.2, f32[3072]{0:T(1024)S(1)} %add_rsqrt_fusion.1, f32[1536]{0:T(1024)S(1)} %broadcast_multiply_fusion), kind=kOutput, calls=%fused_computation.13 | convolution fusion | flops 2436756480 | bytes 14186496 | tf_op jit(solution)/shard_map/dot_general | solution.py:115
  191.1 0.9 constant_dynamic-slice_fusion
  192.1 1.2 copy.7
  (18 shorter events, 3.3 us)
Async XLA Ops:
  6.3 21.1 %all-to-all-start = ((f32[16,1,1536]{2,1,0:T(1,128)}), f32[16,1,1536]{2,1,0:T(1,128)S(1)}, u32[]{:S(2)}, u32[]{:S(2)}) async-start(f32[16,1,1536]{2,1,0:T(1,128)} %broadcast_in_dim.8), calls=%async_computation | async-start | bytes 196608 | tf_op jit(solution)/shard_map/all_to_all | solution.py:70
  27.5 7.6 %copy-start.1 = (f32[1536,128]{1,0:T(8,128)S(1)}, f32[1536,128]{1,0:T(8,128)}, u32[]{:S(2)}) copy-start(f32[1536,128]{1,0:T(8,128)} %param.3) | copy-start | bytes 2359300
  27.5 0.6 copy-start
  28.1 54.1 %all-to-all-start.1 = ((bf16[16,48,1536]{2,1,0:T(8,128)(2,1)}), bf16[16,48,1536]{2,1,0:T(8,128)(2,1)S(1)}, u32[]{:S(2)}, u32[]{:S(2)}) async-start(bf16[16,48,1536]{2,1,0:T(8,128)(2,1)} %bitcast.26), calls=%async_computation.1 | async-start | bytes 4718592 | tf_op jit(solution)/shard_map/all_to_all | solution.py:94
  121.6 16.7 %all-to-all-start.3 = ((bf16[16,48,256]{2,1,0:T(8,128)(2,1)}), bf16[16,48,256]{2,1,0:T(8,128)(2,1)S(1)}, u32[]{:S(2)}, u32[]{:S(2)}) async-start(bf16[16,48,256]{2,1,0:T(8,128)(2,1)} %broadcast_in_dim.10), calls=%async_computation.3 | async-start | bytes 786432 | tf_op jit(solution)/shard_map/all_to_all | solution.py:70
  153.6 16.7 %all-to-all-start.4 = ((bf16[16,48,256]{2,1,0:T(8,128)(2,1)}), bf16[16,48,256]{2,1,0:T(8,128)(2,1)S(1)}, u32[]{:S(2)}, u32[]{:S(2)}) async-start(bf16[16,48,256]{2,1,0:T(8,128)(2,1)} %broadcast_in_dim.11), calls=%async_computation.4 | async-start | bytes 786432 | tf_op jit(solution)/shard_map/all_to_all | solution.py:70

commit v2 on v1

--- a/solution.py
+++ b/solution.py
@@ -18,9 +18,8 @@
     return hi, mid, low
 
 
-def inverse_factor_kernel(gram_ref, inv_ref, work_ref):
-    size = gram_ref.shape[0]
-    work_ref[...] = gram_ref[...]
+def eliminate(inv_ref, work_ref):
+    size = work_ref.shape[0]
     row = lax.broadcasted_iota(jnp.int32, (size, size), 0)
     col = lax.broadcasted_iota(jnp.int32, (size, size), 1)
     inv_ref[...] = (row == col).astype(jnp.float32)
@@ -37,9 +36,10 @@
         scale = jnp.ones((PANEL, LANES), jnp.float32)
         for k in range(PANEL):
             pivot = spread[k][k : k + 1, :]
-            scale = jnp.where(sub == k, lax.rsqrt(pivot), scale)
+            root = lax.rsqrt(pivot)
+            scale = jnp.where(sub == k, root, scale)
             if k + 1 < PANEL:
-                factor = jnp.where(sub > k, spread[k] * (1.0 / pivot), 0.0)
+                factor = jnp.where(sub > k, spread[k] * (root * root), 0.0)
                 pieces = [x - factor * x[k : k + 1, :] for x in pieces]
                 spread = [x if i <= k else x - factor * x[k : k + 1, :] for i, x in enumerate(spread)]
         pieces = [x * scale for x in pieces]
@@ -56,18 +56,56 @@
             inv_ref[end:, :done] = inv_ref[end:, :done] - change[:, count * LANES :]
 
 
-def inverse_factor(gram):
+def gram_of(products):
+    return lax.dot_general(products, products, (((0,), (0,)), ((), ())), preferred_element_type=jnp.float32)
+
+
+def last_kernel(products_ref, inv_ref, work_ref):
+    work_ref[...] = gram_of(products_ref[...])
+    eliminate(inv_ref, work_ref)
+
+
+def sweep_kernel(products_ref, scatter_ref, copies_ref, work_ref, inv_ref):
+    products = products_ref[...]
+    work_ref[...] = gram_of(products)
+    rows = scatter_ref.shape[0]
+    parts = jnp.dot(
+        jnp.concatenate(split3(scatter_ref[...]), axis=0), products, preferred_element_type=jnp.float32
+    )
+    mixed = parts[:rows] + (parts[rows : 2 * rows] + parts[2 * rows :])
+    eliminate(inv_ref, work_ref)
+    following = lax.dot_general(
+        mixed,
+        inv_ref[...],
+        (((1,), (1,)), ((), ())),
+        precision=lax.Precision.HIGHEST,
+        preferred_element_type=jnp.float32,
+    ).astype(jnp.bfloat16)
+    for i in range(copies_ref.shape[0]):
+        copies_ref[i] = following[: copies_ref.shape[1]]
+
+
+def inverse_factor(products):
+    square = (products.shape[1], products.shape[1])
     return pl.pallas_call(
-        inverse_factor_kernel,
-        out_shape=jax.ShapeDtypeStruct(gram.shape, jnp.float32),
-        scratch_shapes=[pltpu.VMEM(gram.shape, jnp.float32)],
-    )(gram)
+        last_kernel,
+        out_shape=jax.ShapeDtypeStruct(square, jnp.float32),
+        scratch_shapes=[pltpu.VMEM(square, jnp.float32)],
+    )(products)
+
+
+def next_copies(products, scatter, parts, piece):
+    square = (products.shape[1], products.shape[1])
+    return pl.pallas_call(
+        sweep_kernel,
+        out_shape=jax.ShapeDtypeStruct((parts, piece, products.shape[1]), jnp.bfloat16),
+        scratch_shapes=[pltpu.VMEM(square, jnp.float32), pltpu.VMEM(square, jnp.float32)],
+    )(products, scatter)
 
 
 def gather_rows(x):
     parts = lax.axis_size("rows")
-    copies = jnp.broadcast_to(x[None], (parts,) + x.shape)
-    return lax.all_to_all(copies, "rows", 0, 0)
+    return lax.all_to_all(jnp.broadcast_to(x[None], (parts,) + x.shape), "rows", 0, 0)
 
 
 def shards(embeddings, start_basis):
@@ -99,25 +137,24 @@
     )
 
     basis = lax.all_gather(start_basis.astype(bf16), "cols", axis=1, tiled=True)
-    next_piece = jnp.dot(scatter, basis.astype(f32), precision=highest)
+    first = jnp.dot(scatter, basis.astype(f32), precision=highest).astype(bf16)
+    copies = jnp.broadcast_to(first[None], (row_parts,) + first.shape)
+    padded = jnp.pad(scatter, ((0, -piece % PANEL), (0, 0)))
     for sweep_index in range(ITERS):
-        own_products = gather_rows(next_piece.astype(bf16)).reshape(half, basis_cols)
+        own_products = lax.all_to_all(copies, "rows", 0, 0).reshape(half, basis_cols)
         products = lax.all_gather(own_products, "cols", axis=0, tiled=True)
-        gram_matrix = lax.dot_general(products, products, (((0,), (0,)), ((), ())), preferred_element_type=f32)
-        inverse = inverse_factor(gram_matrix)
         if sweep_index + 1 < ITERS:
-            mixed = jnp.dot(scatter, products.astype(f32), precision=highest)
-            next_piece = lax.dot_general(mixed, inverse, (((1,), (1,)), ((), ())), precision=highest)
+            copies = next_copies(products, padded, row_parts, piece)
+    inverse = jnp.roll(inverse_factor(products), -col_index * col_block, axis=0)
     basis = lax.dot_general(products.astype(f32), inverse, (((1,), (1,)), ((), ())), precision=highest)
 
     centered = embeddings.astype(f32) - col_mean[None, :]
     unit = (centered * lax.rsqrt(jnp.sum(centered * centered, axis=1, keepdims=True) + 1.0)).astype(bf16)
+    unit = lax.optimization_barrier(unit)
     coords = jnp.dot(unit, basis.astype(bf16), preferred_element_type=f32)
     squares = jnp.sum(coords * coords, axis=1, keepdims=True)
-    own_coords = lax.dynamic_slice_in_dim(coords, col_index * col_block, col_block, 1)
-    scaled = own_coords * lax.rsqrt(squares / basis_cols + 0.0001)
-    own_basis = lax.dynamic_slice_in_dim(basis, col_index * col_block, col_block, 1)
-    return (scaled.astype(bf16), own_basis)
+    scaled = coords[:, :col_block] * lax.rsqrt(squares / basis_cols + 0.0001)
+    return (scaled.astype(bf16), basis[:, :col_block])
 
 
 def solution(mesh):

time: 194 us -> 190 us (0.979)
  blocking collectives: 32.2 us -> 10.5 us
  starting transfers between devices: 22.7 us -> 33.3 us
  other arithmetic: 13.7 us -> 23.2 us
  matrix products: 28.8 us -> 21.3 us
  Pallas kernels: 27.6 us -> 31.2 us
  waiting for transfers between devices: 62.5 us -> 64.9 us
    all_to_all x1 -> x0, blocking collectives: 22.6 us -> none  [gather_rows(): return lax.all_to_all(copies, 'rows', 0, 0)]
    all_to_all x3 -> x4, starting transfers between devices: 15.8 us -> 26.4 us  [the longest x3 18.1 us: shards(): lax.all_to_all(copies, 'rows', 0, 0).reshape(half, basis_cols)]
    convert_element_type x1 -> x2, other arithmetic: 0.11 us -> 9.6 us  [the longest x1 9.48 us: shards(): (centered * lax.rsqrt(jnp.sum(centered * centered, axis=1, keepdims=True)...]
    dot_general x8 -> x1, matrix products: 7.46 us -> 0.51 us  [shards(): first = jnp.dot(scatter, basis.astype(f32), precision=highest).astype(bf16)]
    pallas_call x3, Pallas kernels: 27.6 us -> 31.2 us  [the longest x2 21.3 us: next_copies(): pl.pallas_call(sweep_kernel, out_shape=jax.ShapeDtypeStruct((parts, piece...]
    all_to_all x3 -> x4, waiting for transfers between devices: 19.7 us -> 22.3 us  [the longest x3 22.3 us: shards(): lax.all_to_all(copies, 'rows', 0, 0).reshape(half, basis_cols)]
  transfers between devices with their start and end apart: 4 -> 5, of which waited for: 3 -> 4; matrix products, arithmetic and copies ran while one was open for 11% -> 16% of each run, Pallas kernels for 0% -> 0%
where the time goes in v2:
time: 190 us; the launch traced here: 189 us
  waiting for transfers between devices  64.9 us (34%)
  starting transfers between devices  33.3 us (18%)
  Pallas kernels  31.2 us (16%)
  other arithmetic  23.2 us (12%)
  matrix products  21.3 us (11%)
  blocking collectives  10.5 us (6%)
  local copies, waits for them, and re-layouts  4.2 us (2%)
    all_to_all x1, waiting for transfers between devices, shards(): lax.all_to_all(within.reshape(row_parts, piece, width), 'rows', 0, 0)  42.6 us
    all_to_all x3, waiting for transfers between devices, shards(): lax.all_to_all(copies, 'rows', 0, 0).reshape(half, basis_cols)  22.3 us
    pallas_call x2, Pallas kernels, next_copies(): pl.pallas_call(sweep_kernel, out_shape=jax.ShapeDtypeStruct((parts, piece...  21.3 us
    all_to_all x3, starting transfers between devices, shards(): lax.all_to_all(copies, 'rows', 0, 0).reshape(half, basis_cols)  18.1 us
    dot_general x1, matrix products, shards(): lax.dot_general(own_half, embeddings, (((0,), (0,)), ((), ())), preferred...  12.9 us
    pallas_call x1, Pallas kernels, inverse_factor(): pl.pallas_call(last_kernel, out_shape=jax.ShapeDtypeStruct(square, jnp.fl...  9.93 us
    convert_element_type x1, other arithmetic, shards(): (centered * lax.rsqrt(jnp.sum(centered * centered, axis=1, keepdims=True)...  9.48 us
    all_to_all x1, starting transfers between devices, gather_rows(): lax.all_to_all(jnp.broadcast_to(x[None], (parts,) + x.shape), 'rows', 0, 0)  8.34 us
  transfers between devices with their start and end apart: 5, of which 4 were waited for; matrix products, arithmetic and copies ran while one was open for 16% of the time, Pallas kernels for 0%

profile of v2, /device:TPU:0, one launch (start us, length us, event | category | flops | bytes accessed | tf_op | source)
XLA Modules:
  0.0 189.4 jit_solution(8615667854529775419)
XLA Ops:
  0.6 5.0 %convert_reduce_fusion = f32[1536]{0:T(1024)S(1)} fusion(bf16[3072,1536]{1,0:T(8,128)(2,1)} %param.2), kind=kLoop, calls=%fused_computation.1 | loop fusion | flops 9435648 | bytes 9443328 | tf_op jit(solution)/shard_map/reduce_sum | solution.py:124
  5.7 0.7 broadcast_in_dim.4
  6.3 8.3 %all-to-all-start = ((f32[16,1,1536]{2,1,0:T(1,128)}), f32[16,1,1536]{2,1,0:T(1,128)S(1)}, u32[]{:S(2)}, u32[]{:S(2)}) async-start(f32[16,1,1536]{2,1,0:T(1,128)} %broadcast_in_dim.4), calls=%async_computation | async-start | bytes 196608 | tf_op jit(solution)/shard_map/all_to_all | solution.py:108
  14.8 12.9 %subtract_convert_fusion = bf16[768,1536]{1,0:T(8,128)(2,1)} fusion(bf16[3072,1536]{1,0:T(8,128)(2,1)} %param.2, s32[]{:T(128)S(6)} %select_n.20, f32[1536]{0:T(1024)S(1)} %broadcast_multiply_fusion.1, f32[768]{0:T(1024)S(1)} %dynamic-slice_multiply_fusion), kind=kOutput, calls=%fused_computation.7 | convolution fusion | flops 7251296256 | bytes 16524292 | tf_op jit(solution)/shard_map/dot_general | solution.py:130
  27.7 0.6 copy-done.1
  28.4 6.9 %all-to-all-start.1 = ((bf16[16,48,1536]{2,1,0:T(8,128)(2,1)}), bf16[16,48,1536]{2,1,0:T(8,128)(2,1)S(1)}, u32[]{:S(2)}, u32[]{:S(2)}) async-start(bf16[16,48,1536]{2,1,0:T(8,128)(2,1)} %bitcast.12), calls=%async_computation.1 | async-start | bytes 4718592 | tf_op jit(solution)/shard_map/all_to_all | solution.py:132
  35.3 2.4 %all_gather.12 = bf16[1536,256]{1,0:T(8,128)(2,1)S(1)} all-gather(bf16[1536,128]{1,0:T(8,128)(2,1)S(1)} %convert_element_type.31), channel_id=1, replica_groups=mesh['rows'=16,'cols'=2] {'cols'}, dimensions={1}, use_global_device_ids=true | all-gather | bytes 1179648 | tf_op jit(solution)/shard_map/all_gather | solution.py:139
  37.7 1.0 reduce_sum.46
  38.7 0.9 bitcast_subtract_fusion
  39.6 42.6 %all-to-all-done.1 = bf16[16,48,1536]{2,1,0:T(8,128)(2,1)S(1)} async-done(((bf16[16,48,1536]{2,1,0:T(8,128)(2,1)}), bf16[16,48,1536]{2,1,0:T(8,128)(2,1)S(1)}, u32[]{:S(2)}, u32[]{:S(2)}) %all-to-all-start.1) | async-done | bytes 2359328 | tf_op jit(solution)/shard_map/all_to_all | solution.py:132
  82.3 0.3 convert_reduce_fusion.1
  82.6 0.5 fusion.8.scatter_ref
  83.1 0.5 convolution_convert_fusion
  83.6 0.8 broadcast_in_dim.5
  84.4 10.8 %all-to-all-start.2 = ((bf16[16,48,256]{2,1,0:T(8,128)(2,1)}), bf16[16,48,256]{2,1,0:T(8,128)(2,1)S(1)}, u32[]{:S(2)}, u32[]{:S(2)}) async-start(bf16[16,48,256]{2,1,0:T(8,128)(2,1)} %broadcast_in_dim.5), calls=%async_computation.2 | async-start | bytes 786432 | tf_op jit(solution)/shard_map/all_to_all | solution.py:144
  95.3 11.8 %all-to-all-done.2 = bf16[16,48,256]{2,1,0:T(8,128)(2,1)S(1)} async-done(((bf16[16,48,256]{2,1,0:T(8,128)(2,1)}), bf16[16,48,256]{2,1,0:T(8,128)(2,1)S(1)}, u32[]{:S(2)}, u32[]{:S(2)}) %all-to-all-start.2) | async-done | bytes 393248 | tf_op jit(solution)/shard_map/all_to_all | solution.py:144
  107.1 2.7 %all_gather.13.products_ref = bf16[1536,256]{1,0:T(8,128)(2,1)} all-gather(bf16[768,256]{1,0:T(8,128)(2,1)S(1)} %bitcast.13), channel_id=1, replica_groups=mesh['rows'=16,'cols'=2] {'cols'}, dimensions={0}, use_global_device_ids=true | all-gather | bytes 1179648 | tf_op jit(solution)/shard_map/all_gather | solution.py:145
  109.8 10.6 %shard_map.41 = bf16[16,48,256]{2,1,0:T(8,128)(2,1)} custom-call(bf16[1536,256]{1,0:T(8,128)(2,1)} %all_gather.13.products_ref, f32[48,1536]{1,0:T(8,128)} %copy-done), custom_call_target="tpu_custom_call" | custom-call | tf_op jit(solution)/shard_map/pallas_call | solution.py:99
  120.4 3.6 %all-to-all-start.3 = ((bf16[16,48,256]{2,1,0:T(8,128)(2,1)}), bf16[16,48,256]{2,1,0:T(8,128)(2,1)S(1)}, u32[]{:S(2)}, u32[]{:S(2)}) async-start(bf16[16,48,256]{2,1,0:T(8,128)(2,1)} %shard_map.41), calls=%async_computation.3 | async-start | bytes 786432 | tf_op jit(solution)/shard_map/all_to_all | solution.py:144
  124.1 6.2 %fusion.2 = f32[3072]{0:T(1024)S(1)} fusion(bf16[3072,1536]{1,0:T(8,128)(2,1)} %param.2, f32[1536]{0:T(1024)S(1)} %broadcast_multiply_fusion), kind=kLoop, calls=%fused_computation.4 | loop fusion | flops 18871296 | bytes 9455616 | tf_op jit(solution)/shard_map/reduce_sum | solution.py:152
  130.3 6.8 %all-to-all-done.3 = bf16[16,48,256]{2,1,0:T(8,128)(2,1)S(1)} async-done(((bf16[16,48,256]{2,1,0:T(8,128)(2,1)}), bf16[16,48,256]{2,1,0:T(8,128)(2,1)S(1)}, u32[]{:S(2)}, u32[]{:S(2)}) %all-to-all-start.3) | async-done | bytes 393248 | tf_op jit(solution)/shard_map/all_to_all | solution.py:144
  137.1 2.7 %all_gather.14.products_ref = bf16[1536,256]{1,0:T(8,128)(2,1)} all-gather(bf16[768,256]{1,0:T(8,128)(2,1)S(1)} %bitcast.14), channel_id=1, replica_groups=mesh['rows'=16,'cols'=2] {'cols'}, dimensions={0}, use_global_device_ids=true | all-gather | bytes 1179648 | tf_op jit(solution)/shard_map/all_gather | solution.py:145
  139.8 10.6 %shard_map.42 = bf16[16,48,256]{2,1,0:T(8,128)(2,1)} custom-call(bf16[1536,256]{1,0:T(8,128)(2,1)} %all_gather.14.products_ref, f32[48,1536]{1,0:T(8,128)} %copy-done), custom_call_target="tpu_custom_call" | custom-call | tf_op jit(solution)/shard_map/pallas_call | solution.py:99
  150.5 3.6 %all-to-all-start.4 = ((bf16[16,48,256]{2,1,0:T(8,128)(2,1)}), bf16[16,48,256]{2,1,0:T(8,128)(2,1)S(1)}, u32[]{:S(2)}, u32[]{:S(2)}) async-start(bf16[16,48,256]{2,1,0:T(8,128)(2,1)} %shard_map.42), calls=%async_computation.4 | async-start | bytes 786432 | tf_op jit(solution)/shard_map/all_to_all | solution.py:144
  154.1 9.5 %fusion.3 = bf16[3072,1536]{1,0:T(8,128)(2,1)} fusion(bf16[3072,1536]{1,0:T(8,128)(2,1)} %param.2, f32[3072]{0:T(1024)S(1)} %add_rsqrt_fusion.1, f32[1536]{0:T(1024)S(1)} %broadcast_multiply_fusion), kind=kLoop, calls=%fused_computation.5 | loop fusion | flops 18874368 | bytes 18892800 | tf_op jit(solution)/shard_map/convert_element_type | solution.py:152
  163.6 3.6 %all-to-all-done.4 = bf16[16,48,256]{2,1,0:T(8,128)(2,1)S(1)} async-done(((bf16[16,48,256]{2,1,0:T(8,128)(2,1)}), bf16[16,48,256]{2,1,0:T(8,128)(2,1)S(1)}, u32[]{:S(2)}, u32[]{:S(2)}) %all-to-all-start.4) | async-done | bytes 393248 | tf_op jit(solution)/shard_map/all_to_all | solution.py:144
  167.1 2.7 %all_gather.15.products_ref = bf16[1536,256]{1,0:T(8,128)(2,1)} all-gather(bf16[768,256]{1,0:T(8,128)(2,1)S(1)} %bitcast.15), channel_id=1, replica_groups=mesh['rows'=16,'cols'=2] {'cols'}, dimensions={0}, use_global_device_ids=true | all-gather | bytes 1179648 | tf_op jit(solution)/shard_map/all_gather | solution.py:145
  169.9 9.9 %shard_map.43 = f32[256,256]{1,0:T(8,128)} custom-call(bf16[1536,256]{1,0:T(8,128)(2,1)} %all_gather.15.products_ref), custom_call_target="tpu_custom_call" | custom-call | tf_op jit(solution)/shard_map/pallas_call | solution.py:90
  179.8 2.0 %fusion.13 = f32[1536,256]{1,0:T(8,128)S(1)} fusion(bf16[1536,256]{1,0:T(8,128)(2,1)} %all_gather.15.products_ref, s32[]{:T(128)S(6)} %select_n.23, f32[256,256]{1,0:T(8,128)} %shard_map.43), kind=kOutput, calls=%fused_computation.21 | convolution fusion | flops 1208025088 | bytes 2621444 | tf_op jit(solution)/shard_map/dot_general | solution.py:149
  181.9 0.9 slice.9
  182.8 5.3 %multiply_reduce_fusion = (f32[3072]{0:T(1024)S(1)}, f32[3072,256]{0,1:T(8,128)S(1)}) fusion(bf16[3072,1536]{1,0:T(8,128)(2,1)} %fusion.3, f32[1536,256]{1,0:T(8,128)S(1)} %fusion.13), kind=kOutput, calls=%fused_computation.10 | convolution fusion | flops 2417882112 | bytes 14168064 | tf_op jit(solution)/shard_map/dot_general | solution.py:154
  188.3 1.2 copy.7
  (13 shorter events, 0.3 us)
Async XLA Ops:
  6.3 21.4 %all-to-all-start = ((f32[16,1,1536]{2,1,0:T(1,128)}), f32[16,1,1536]{2,1,0:T(1,128)S(1)}, u32[]{:S(2)}, u32[]{:S(2)}) async-start(f32[16,1,1536]{2,1,0:T(1,128)} %broadcast_in_dim.4), calls=%async_computation | async-start | bytes 196608 | tf_op jit(solution)/shard_map/all_to_all | solution.py:108
  14.8 20.5 %copy-start.2 = (f32[1536,128]{1,0:T(8,128)S(1)}, f32[1536,128]{1,0:T(8,128)}, u32[]{:S(2)}) copy-start(f32[1536,128]{1,0:T(8,128)} %param.3) | copy-start | bytes 2359300
  27.7 0.6 copy-start.1
  28.4 53.9 %all-to-all-start.1 = ((bf16[16,48,1536]{2,1,0:T(8,128)(2,1)}), bf16[16,48,1536]{2,1,0:T(8,128)(2,1)S(1)}, u32[]{:S(2)}, u32[]{:S(2)}) async-start(bf16[16,48,1536]{2,1,0:T(8,128)(2,1)} %bitcast.12), calls=%async_computation.1 | async-start | bytes 4718592 | tf_op jit(solution)/shard_map/all_to_all | solution.py:132
  83.1 26.7 %copy-start = (f32[48,1536]{1,0:T(8,128)}, f32[48,1536]{1,0:T(8,128)S(1)}, u32[]{:S(2)}) copy-start(f32[48,1536]{1,0:T(8,128)S(1)} %fusion.8.scatter_ref) | copy-start | bytes 884740
  84.4 22.7 %all-to-all-start.2 = ((bf16[16,48,256]{2,1,0:T(8,128)(2,1)}), bf16[16,48,256]{2,1,0:T(8,128)(2,1)S(1)}, u32[]{:S(2)}, u32[]{:S(2)}) async-start(bf16[16,48,256]{2,1,0:T(8,128)(2,1)} %broadcast_in_dim.5), calls=%async_computation.2 | async-start | bytes 786432 | tf_op jit(solution)/shard_map/all_to_all | solution.py:144
  120.4 16.7 %all-to-all-start.3 = ((bf16[16,48,256]{2,1,0:T(8,128)(2,1)}), bf16[16,48,256]{2,1,0:T(8,128)(2,1)S(1)}, u32[]{:S(2)}, u32[]{:S(2)}) async-start(bf16[16,48,256]{2,1,0:T(8,128)(2,1)} %shard_map.41), calls=%async_computation.3 | async-start | bytes 786432 | tf_op jit(solution)/shard_map/all_to_all | solution.py:144
  150.5 16.7 %all-to-all-start.4 = ((bf16[16,48,256]{2,1,0:T(8,128)(2,1)}), bf16[16,48,256]{2,1,0:T(8,128)(2,1)S(1)}, u32[]{:S(2)}, u32[]{:S(2)}) async-start(bf16[16,48,256]{2,1,0:T(8,128)(2,1)} %shard_map.42), calls=%async_computation.4 | async-start | bytes 786432 | tf_op jit(solution)/shard_map/all_to_all | solution.py:144

commit v3 on v2

--- a/solution.py
+++ b/solution.py
@@ -7,6 +7,7 @@
 
 ITERS = 3
 PANEL = 16
+CUTS = 2
 LANES = 128
 
 
@@ -127,12 +128,19 @@
 
     own_half = lax.dynamic_slice_in_dim(embeddings, col_index * half, half, 1)
     own_half_mean = lax.dynamic_slice_in_dim(own_mean, col_index * half, half, 0)
-    second = lax.dot_general(own_half, embeddings, (((0,), (0,)), ((), ())), preferred_element_type=f32)
-    within = (second - (local_rows * own_half_mean)[:, None] * own_mean[None, :]).astype(bf16)
-    received = lax.all_to_all(within.reshape(row_parts, piece, width), "rows", 0, 0)
+    scaled_mean = (local_rows * own_half_mean)[:, None]
+    received = []
+    for cut in range(CUTS):
+        span = slice(cut * width // CUTS, (cut + 1) * width // CUTS)
+        second = lax.dot_general(
+            own_half, embeddings[:, span], (((0,), (0,)), ((), ())), preferred_element_type=f32
+        )
+        within = (second - scaled_mean * own_mean[None, span]).astype(bf16)
+        received.append(lax.all_to_all(within.reshape(row_parts, piece, -1), "rows", 0, 0))
     between = means - col_mean[None, :]
     own_between = lax.dynamic_slice_in_dim(between, col_index * half + row_index * piece, piece, 1)
-    scatter = jnp.sum(received.astype(f32), axis=0) + local_rows * lax.dot_general(
+    within_sum = jnp.concatenate([jnp.sum(x.astype(f32), axis=0) for x in received], axis=1)
+    scatter = within_sum + local_rows * lax.dot_general(
         own_between, between, (((0,), (0,)), ((), ())), precision=highest
     )
 

time: 190 us -> 192 us (1.011)
  matrix products: 21.3 us -> 26 us
  waiting for transfers between devices: 64.9 us -> 60.5 us
    all_to_all x1 -> x2, starting transfers between devices: 6.9 us -> 13.1 us  [shards(): lax.all_to_all(within.reshape(row_parts, piece, -1), 'rows', 0, 0)]
    dot_general x1 -> x2, matrix products: 12.9 us -> 17.7 us  [shards(): lax.dot_general(own_half, embeddings[:, span], (((0,), (0,)), ((), ())),...]
    all_to_all x3, starting transfers between devices: 18.1 us -> 13.4 us  [shards(): lax.all_to_all(copies, 'rows', 0, 0).reshape(half, basis_cols)]
    all_to_all x1 -> x2, waiting for transfers between devices: 42.6 us -> 38.7 us  [shards(): lax.all_to_all(within.reshape(row_parts, piece, -1), 'rows', 0, 0)]
  transfers between devices with their start and end apart: 5 -> 6, of which waited for: 4 -> 5; matrix products, arithmetic and copies ran while one was open for 16% -> 19% of each run, Pallas kernels for 0% -> 0%
where the time goes in v3:
time: 192 us; the launch traced here: 191 us
  waiting for transfers between devices  60.5 us (32%)
  starting transfers between devices  34.7 us (18%)
  Pallas kernels  31.2 us (16%)
  matrix products  26 us (14%)
  other arithmetic  23.1 us (12%)
  blocking collectives  10.5 us (5%)
  local copies, waits for them, and re-layouts  4.2 us (2%)
    all_to_all x2, waiting for transfers between devices, shards(): lax.all_to_all(within.reshape(row_parts, piece, -1), 'rows', 0, 0)  38.7 us
    all_to_all x3, waiting for transfers between devices, shards(): lax.all_to_all(copies, 'rows', 0, 0).reshape(half, basis_cols)  21.8 us
    pallas_call x2, Pallas kernels, next_copies(): pl.pallas_call(sweep_kernel, out_shape=jax.ShapeDtypeStruct((parts, piece...  21.3 us
    dot_general x2, matrix products, shards(): lax.dot_general(own_half, embeddings[:, span], (((0,), (0,)), ((), ())),...  17.7 us
    all_to_all x3, starting transfers between devices, shards(): lax.all_to_all(copies, 'rows', 0, 0).reshape(half, basis_cols)  13.4 us
    all_to_all x2, starting transfers between devices, shards(): lax.all_to_all(within.reshape(row_parts, piece, -1), 'rows', 0, 0)  13.1 us
    pallas_call x1, Pallas kernels, inverse_factor(): pl.pallas_call(last_kernel, out_shape=jax.ShapeDtypeStruct(square, jnp.fl...  9.93 us
    convert_element_type x1, other arithmetic, shards(): (centered * lax.rsqrt(jnp.sum(centered * centered, axis=1, keepdims=True)...  9.48 us
  transfers between devices with their start and end apart: 6, of which 5 were waited for; matrix products, arithmetic and copies ran while one was open for 19% of the time, Pallas kernels for 0%

profile of v3, /device:TPU:0, one launch (start us, length us, event | category | flops | bytes accessed | tf_op | source)
XLA Modules:
  0.0 191.2 jit_solution(13756813374539697958)
XLA Ops:
  0.6 5.0 %convert_reduce_fusion = f32[1536]{0:T(1024)S(1)} fusion(bf16[3072,1536]{1,0:T(8,128)(2,1)} %param.2), kind=kLoop, calls=%fused_computation.1 | loop fusion | flops 9435648 | bytes 9443328 | tf_op jit(solution)/shard_map/reduce_sum | solution.py:125
  5.7 0.7 broadcast_in_dim.4
  6.3 8.3 %all-to-all-start = ((f32[16,1,1536]{2,1,0:T(1,128)}), f32[16,1,1536]{2,1,0:T(1,128)S(1)}, u32[]{:S(2)}, u32[]{:S(2)}) async-start(f32[16,1,1536]{2,1,0:T(1,128)} %broadcast_in_dim.4), calls=%async_computation | async-start | bytes 196608 | tf_op jit(solution)/shard_map/all_to_all | solution.py:109
  14.8 8.7 %subtract_convert_fusion = bf16[768,768]{1,0:T(8,128)(2,1)} fusion(bf16[3072,1536]{1,0:T(8,128)(2,1)} %param.2, s32[]{:T(128)S(6)} %select_n.20, f32[768]{0:T(1024)S(1)} %get-tuple-element.9, f32[768]{0:T(1024)S(1)} %get-tuple-element.10), kind=kOutput, calls=%fused_computation.14 | convolution fusion | flops 3625648128 | bytes 10622980 | tf_op jit(solution)/shard_map/dot_general | solution.py:135
  23.5 0.6 copy-done.1
  24.1 6.9 %all-to-all-start.2 = ((bf16[16,48,768]{2,1,0:T(8,128)(2,1)}), bf16[16,48,768]{2,1,0:T(8,128)(2,1)S(1)}, u32[]{:S(2)}, u32[]{:S(2)}) async-start(bf16[16,48,768]{2,1,0:T(8,128)(2,1)} %bitcast.1), calls=%async_computation.2 | async-start | bytes 2359296 | tf_op jit(solution)/shard_map/all_to_all | solution.py:139
  31.0 9.0 %subtract_convert_fusion.1 = bf16[768,768]{1,0:T(8,128)(2,1)} fusion(bf16[3072,1536]{1,0:T(8,128)(2,1)} %param.2, s32[]{:T(128)S(6)} %select_n.20, f32[768]{0:T(1024)S(1)} %get-tuple-element.8, f32[768]{0:T(1024)S(1)} %get-tuple-element.10), kind=kOutput, calls=%fused_computation.16 | convolution fusion | flops 3625648128 | bytes 10622980 | tf_op jit(solution)/shard_map/dot_general | solution.py:135
  40.0 17.5 %all-to-all-done.2 = bf16[16,48,768]{2,1,0:T(8,128)(2,1)S(1)} async-done(((bf16[16,48,768]{2,1,0:T(8,128)(2,1)}), bf16[16,48,768]{2,1,0:T(8,128)(2,1)S(1)}, u32[]{:S(2)}, u32[]{:S(2)}) %all-to-all-start.2) | async-done | bytes 1179680 | tf_op jit(solution)/shard_map/all_to_all | solution.py:139
  57.5 6.2 %all-to-all-start.1 = ((bf16[16,48,768]{2,1,0:T(8,128)(2,1)}), bf16[16,48,768]{2,1,0:T(8,128)(2,1)S(1)}, u32[]{:S(2)}, u32[]{:S(2)}) async-start(bf16[16,48,768]{2,1,0:T(8,128)(2,1)} %bitcast), calls=%async_computation.1 | async-start | bytes 2359296 | tf_op jit(solution)/shard_map/all_to_all | solution.py:139
  63.7 2.4 %all_gather.12 = bf16[1536,256]{1,0:T(8,128)(2,1)S(1)} all-gather(bf16[1536,128]{1,0:T(8,128)(2,1)S(1)} %convert_element_type.39), channel_id=1, replica_groups=mesh['rows'=16,'cols'=2] {'cols'}, dimensions={1}, use_global_device_ids=true | all-gather | bytes 1179648 | tf_op jit(solution)/shard_map/all_gather | solution.py:147
  66.1 1.0 reduce_sum.55
  67.1 0.9 bitcast_subtract_fusion
  68.2 21.2 %all-to-all-done.1 = bf16[16,48,768]{2,1,0:T(8,128)(2,1)S(1)} async-done(((bf16[16,48,768]{2,1,0:T(8,128)(2,1)}), bf16[16,48,768]{2,1,0:T(8,128)(2,1)S(1)}, u32[]{:S(2)}, u32[]{:S(2)}) %all-to-all-start.1) | async-done | bytes 1179680 | tf_op jit(solution)/shard_map/all_to_all | solution.py:139
  90.6 0.8 broadcast_in_dim.5
  91.4 6.1 %all-to-all-start.3 = ((bf16[16,48,256]{2,1,0:T(8,128)(2,1)}), bf16[16,48,256]{2,1,0:T(8,128)(2,1)S(1)}, u32[]{:S(2)}, u32[]{:S(2)}) async-start(bf16[16,48,256]{2,1,0:T(8,128)(2,1)} %broadcast_in_dim.5), calls=%async_computation.3 | async-start | bytes 786432 | tf_op jit(solution)/shard_map/all_to_all | solution.py:152
  97.5 11.4 %all-to-all-done.3 = bf16[16,48,256]{2,1,0:T(8,128)(2,1)S(1)} async-done(((bf16[16,48,256]{2,1,0:T(8,128)(2,1)}), bf16[16,48,256]{2,1,0:T(8,128)(2,1)S(1)}, u32[]{:S(2)}, u32[]{:S(2)}) %all-to-all-start.3) | async-done | bytes 393248 | tf_op jit(solution)/shard_map/all_to_all | solution.py:152
  108.9 2.7 %all_gather.13.products_ref = bf16[1536,256]{1,0:T(8,128)(2,1)} all-gather(bf16[768,256]{1,0:T(8,128)(2,1)S(1)} %bitcast.12), channel_id=1, replica_groups=mesh['rows'=16,'cols'=2] {'cols'}, dimensions={0}, use_global_device_ids=true | all-gather | bytes 1179648 | tf_op jit(solution)/shard_map/all_gather | solution.py:153
  111.6 10.6 %shard_map.41 = bf16[16,48,256]{2,1,0:T(8,128)(2,1)} custom-call(bf16[1536,256]{1,0:T(8,128)(2,1)} %all_gather.13.products_ref, f32[48,1536]{1,0:T(8,128)} %copy-done), custom_call_target="tpu_custom_call" | custom-call | tf_op jit(solution)/shard_map/pallas_call | solution.py:100
  122.3 3.6 %all-to-all-start.4 = ((bf16[16,48,256]{2,1,0:T(8,128)(2,1)}), bf16[16,48,256]{2,1,0:T(8,128)(2,1)S(1)}, u32[]{:S(2)}, u32[]{:S(2)}) async-start(bf16[16,48,256]{2,1,0:T(8,128)(2,1)} %shard_map.41), calls=%async_computation.4 | async-start | bytes 786432 | tf_op jit(solution)/shard_map/all_to_all | solution.py:152
  125.9 6.2 %fusion.2 = f32[3072]{0:T(1024)S(1)} fusion(bf16[3072,1536]{1,0:T(8,128)(2,1)} %param.2, f32[1536]{0:T(1024)S(1)} %broadcast_multiply_fusion), kind=kLoop, calls=%fused_computation.4 | loop fusion | flops 18871296 | bytes 9455616 | tf_op jit(solution)/shard_map/reduce_sum | solution.py:160
  132.1 6.8 %all-to-all-done.4 = bf16[16,48,256]{2,1,0:T(8,128)(2,1)S(1)} async-done(((bf16[16,48,256]{2,1,0:T(8,128)(2,1)}), bf16[16,48,256]{2,1,0:T(8,128)(2,1)S(1)}, u32[]{:S(2)}, u32[]{:S(2)}) %all-to-all-start.4) | async-done | bytes 393248 | tf_op jit(solution)/shard_map/all_to_all | solution.py:152
  138.9 2.7 %all_gather.14.products_ref = bf16[1536,256]{1,0:T(8,128)(2,1)} all-gather(bf16[768,256]{1,0:T(8,128)(2,1)S(1)} %bitcast.13), channel_id=1, replica_groups=mesh['rows'=16,'cols'=2] {'cols'}, dimensions={0}, use_global_device_ids=true | all-gather | bytes 1179648 | tf_op jit(solution)/shard_map/all_gather | solution.py:153
  141.6 10.6 %shard_map.42 = bf16[16,48,256]{2,1,0:T(8,128)(2,1)} custom-call(bf16[1536,256]{1,0:T(8,128)(2,1)} %all_gather.14.products_ref, f32[48,1536]{1,0:T(8,128)} %copy-done), custom_call_target="tpu_custom_call" | custom-call | tf_op jit(solution)/shard_map/pallas_call | solution.py:100
  152.3 3.6 %all-to-all-start.5 = ((bf16[16,48,256]{2,1,0:T(8,128)(2,1)}), bf16[16,48,256]{2,1,0:T(8,128)(2,1)S(1)}, u32[]{:S(2)}, u32[]{:S(2)}) async-start(bf16[16,48,256]{2,1,0:T(8,128)(2,1)} %shard_map.42), calls=%async_computation.5 | async-start | bytes 786432 | tf_op jit(solution)/shard_map/all_to_all | solution.py:152
  155.9 9.5 %fusion.3 = bf16[3072,1536]{1,0:T(8,128)(2,1)} fusion(bf16[3072,1536]{1,0:T(8,128)(2,1)} %param.2, f32[3072]{0:T(1024)S(1)} %add_rsqrt_fusion.1, f32[1536]{0:T(1024)S(1)} %broadcast_multiply_fusion), kind=kLoop, calls=%fused_computation.5 | loop fusion | flops 18874368 | bytes 18892800 | tf_op jit(solution)/shard_map/convert_element_type | solution.py:160
  165.4 3.6 %all-to-all-done.5 = bf16[16,48,256]{2,1,0:T(8,128)(2,1)S(1)} async-done(((bf16[16,48,256]{2,1,0:T(8,128)(2,1)}), bf16[16,48,256]{2,1,0:T(8,128)(2,1)S(1)}, u32[]{:S(2)}, u32[]{:S(2)}) %all-to-all-start.5) | async-done | bytes 393248 | tf_op jit(solution)/shard_map/all_to_all | solution.py:152
  169.0 2.7 %all_gather.15.products_ref = bf16[1536,256]{1,0:T(8,128)(2,1)} all-gather(bf16[768,256]{1,0:T(8,128)(2,1)S(1)} %bitcast.14), channel_id=1, replica_groups=mesh['rows'=16,'cols'=2] {'cols'}, dimensions={0}, use_global_device_ids=true | all-gather | bytes 1179648 | tf_op jit(solution)/shard_map/all_gather | solution.py:153
  171.7 9.9 %shard_map.43 = f32[256,256]{1,0:T(8,128)} custom-call(bf16[1536,256]{1,0:T(8,128)(2,1)} %all_gather.15.products_ref), custom_call_target="tpu_custom_call" | custom-call | tf_op jit(solution)/shard_map/pallas_call | solution.py:91
  181.7 2.0 %fusion.23 = f32[1536,256]{1,0:T(8,128)S(1)} fusion(bf16[1536,256]{1,0:T(8,128)(2,1)} %all_gather.15.products_ref, s32[]{:T(128)S(6)} %select_n.23, f32[256,256]{1,0:T(8,128)} %shard_map.43), kind=kOutput, calls=%fused_computation.27 | convolution fusion | flops 1208025088 | bytes 2621444 | tf_op jit(solution)/shard_map/dot_general | solution.py:157
  183.7 0.9 slice.27
  184.6 5.3 %multiply_reduce_fusion = (f32[3072]{0:T(1024)S(1)}, f32[3072,256]{0,1:T(8,128)S(1)}) fusion(bf16[3072,1536]{1,0:T(8,128)(2,1)} %fusion.3, f32[1536,256]{1,0:T(8,128)S(1)} %fusion.23), kind=kOutput, calls=%fused_computation.12 | convolution fusion | flops 2417882112 | bytes 14168064 | tf_op jit(solution)/shard_map/dot_general | solution.py:162
  190.1 1.2 copy.7
  (17 shorter events, 1.6 us)
Async XLA Ops:
  6.3 17.1 %all-to-all-start = ((f32[16,1,1536]{2,1,0:T(1,128)}), f32[16,1,1536]{2,1,0:T(1,128)S(1)}, u32[]{:S(2)}, u32[]{:S(2)}) async-start(f32[16,1,1536]{2,1,0:T(1,128)} %broadcast_in_dim.4), calls=%async_computation | async-start | bytes 196608 | tf_op jit(solution)/shard_map/all_to_all | solution.py:109
  23.5 0.6 copy-start.1
  24.1 33.4 %all-to-all-start.2 = ((bf16[16,48,768]{2,1,0:T(8,128)(2,1)}), bf16[16,48,768]{2,1,0:T(8,128)(2,1)S(1)}, u32[]{:S(2)}, u32[]{:S(2)}) async-start(bf16[16,48,768]{2,1,0:T(8,128)(2,1)} %bitcast.1), calls=%async_computation.2 | async-start | bytes 2359296 | tf_op jit(solution)/shard_map/all_to_all | solution.py:139
  31.0 32.6 %copy-start.2 = (f32[1536,128]{1,0:T(8,128)S(1)}, f32[1536,128]{1,0:T(8,128)}, u32[]{:S(2)}) copy-start(f32[1536,128]{1,0:T(8,128)} %param.3) | copy-start | bytes 2359300
  57.5 31.9 %all-to-all-start.1 = ((bf16[16,48,768]{2,1,0:T(8,128)(2,1)}), bf16[16,48,768]{2,1,0:T(8,128)(2,1)S(1)}, u32[]{:S(2)}, u32[]{:S(2)}) async-start(bf16[16,48,768]{2,1,0:T(8,128)(2,1)} %bitcast), calls=%async_computation.1 | async-start | bytes 2359296 | tf_op jit(solution)/shard_map/all_to_all | solution.py:139
  90.1 21.5 %copy-start = (f32[48,1536]{1,0:T(8,128)}, f32[48,1536]{1,0:T(8,128)S(1)}, u32[]{:S(2)}) copy-start(f32[48,1536]{1,0:T(8,128)S(1)} %fusion.10.scatter_ref) | copy-start | bytes 884740
  91.4 17.6 %all-to-all-start.3 = ((bf16[16,48,256]{2,1,0:T(8,128)(2,1)}), bf16[16,48,256]{2,1,0:T(8,128)(2,1)S(1)}, u32[]{:S(2)}, u32[]{:S(2)}) async-start(bf16[16,48,256]{2,1,0:T(8,128)(2,1)} %broadcast_in_dim.5), calls=%async_computation.3 | async-start | bytes 786432 | tf_op jit(solution)/shard_map/all_to_all | solution.py:152
  122.3 16.7 %all-to-all-start.4 = ((bf16[16,48,256]{2,1,0:T(8,128)(2,1)}), bf16[16,48,256]{2,1,0:T(8,128)(2,1)S(1)}, u32[]{:S(2)}, u32[]{:S(2)}) async-start(bf16[16,48,256]{2,1,0:T(8,128)(2,1)} %shard_map.41), calls=%async_computation.4 | async-start | bytes 786432 | tf_op jit(solution)/shard_map/all_to_all | solution.py:152
  152.3 16.7 %all-to-all-start.5 = ((bf16[16,48,256]{2,1,0:T(8,128)(2,1)}), bf16[16,48,256]{2,1,0:T(8,128)(2,1)S(1)}, u32[]{:S(2)}, u32[]{:S(2)}) async-start(bf16[16,48,256]{2,1,0:T(8,128)(2,1)} %shard_map.42), calls=%async_computation.5 | async-start | bytes 786432 | tf_op jit(solution)/shard_map/all_to_all | solution.py:152
